TPU v7x, 1024 devices: a whole 8x8x8 slice. The times are simulated.
1024 devices in a mesh: img: 64 (over x, z), tile: 16 (over y, core).
Axes of the slice: x: 8, y: 8, z: 8, core: 2. Of those that a mesh axis runs over, the one named last changes fastest.
Arguments:
- query: bfloat16 [64, 2048, 1280], P('img', 'tile'), may hold values from -6 to 6
- keys: bfloat16 [64, 2048, 1280], P('img', 'tile'), may hold values from -6 to 6
- values: bfloat16 [64, 2048, 1280], P('img', 'tile'), may hold values from -6 to 6
- out_weight: bfloat16 [1280, 1280], P('tile'), may hold values from -0.15625 to 0.15625
- hidden: bfloat16 [64, 2048, 1280], P('img', 'tile'), may hold values from -36 to 36
- gain: float32 [1280], replicated, may hold values from 0.5 to 1.5
- seq_grad: bfloat16 [64, 2048, 5120], P('img', 'tile'), may hold values from -6 to 6
- splice_at: int32 [64, 512], P('img', 'tile'), may hold values from 0 to 2047, as said below
- merged_count: int32 [64], P('img'), may hold values from 64 to 512
Outputs:
- query_grad: bfloat16 [64, 2048, 1280], P('img', 'tile')
- key_grad: bfloat16 [64, 2048, 1280], P('img', 'tile')
- value_grad: bfloat16 [64, 2048, 1280], P('img', 'tile')
- gain_grad: float32 [1280], replicated
Inputs may be any that keep to these rules, and one draw needn't show every extreme that they name: `splice_at`: within one image the positions are distinct. The merged rows of one device (aligned blocks of 32 rows) place at most 4 rows in any one block of 128 positions of the sequence.
All inputs are finite; a program needn't handle non-finite values.
Results may differ from a plain program's by a relative error of at most 0.009.
Values may be sent and summed in bfloat16 or wider, within the bound.
A program may use at most 32 MiB of HBM per device.

v0:
```python
import jax
import jax.numpy as jnp
from jax import lax
from jax.sharding import Mesh
from jax.sharding import PartitionSpec as P

TILE = ("tile_0", "tile_1")
IMG_TILE = ("img_0", "img_1", "tile_0", "tile_1")
IMG = ("img_0", "img_1")


norm_eps = 1e-06


def sent_together(arrays, axis, split_dim, concat_dim, along):
    ends, at = ([], 0)
    for a in arrays[:-1]:
        at += a.shape[along]
        ends.append(at)
    both = jnp.concatenate(arrays, axis=along)
    return tuple(
        jnp.split(
            lax.all_to_all(both, axis, split_axis=split_dim, concat_axis=concat_dim, tiled=True),
            ends,
            axis=along,
        )
    )


def by_axis(x, axes):
    for axis in axes:
        x = lax.psum(x, axis)
    return x


def splice_back(seq_grad, splice_at, merged_count, width):
    seq_rows = seq_grad[0]
    span_len = seq_rows.shape[0]
    tile_count = lax.axis_size(TILE)
    my_tile = lax.axis_index(TILE)
    positions = splice_at[0]
    rows_here = positions.shape[0]
    capacity = 2 * rows_here // tile_count
    owners = positions // span_len
    within = positions % span_len
    onehot = (owners[:, None] == jnp.arange(tile_count, dtype=jnp.int32)[None, :]).astype(jnp.int32)
    before = jnp.cumsum(onehot, axis=0) - onehot
    rank_in = jnp.sum(before * onehot, axis=1)
    slot_ids = owners * capacity + rank_in
    requests = jnp.full((tile_count * capacity,), -1, jnp.int32).at[slot_ids].set(within)
    requests = requests.reshape(tile_count, capacity)
    asked_for = lax.all_to_all(requests, TILE, split_axis=0, concat_axis=0, tiled=True)
    found_rows = jnp.take(seq_rows, jnp.clip(asked_for, 0, span_len - 1), axis=0)
    found_rows = jnp.where(
        (asked_for >= 0)[:, :, None], found_rows, jnp.zeros((), found_rows.dtype)
    )
    replies = lax.all_to_all(found_rows, TILE, split_axis=0, concat_axis=0, tiled=True)
    merged = replies.reshape(tile_count * capacity, -1)[slot_ids]
    live_rows = my_tile * rows_here + jnp.arange(rows_here) < merged_count[0]
    merged = jnp.where(live_rows[:, None], merged, jnp.zeros((), merged.dtype))
    return merged.reshape(-1, width)


def norm_backward(hidden, gain, patch_grad):
    values32 = hidden[0].astype(jnp.float32)
    inverse = lax.rsqrt(jnp.mean(values32 * values32, axis=-1, keepdims=True) + norm_eps)
    normed = values32 * inverse
    upstream = patch_grad.astype(jnp.float32)
    gain_part = jnp.sum(upstream * normed, axis=0)
    scaled = gain * upstream
    attn_grad = (
        inverse * (scaled - normed * jnp.mean(scaled * normed, axis=-1, keepdims=True))
    ).astype(jnp.bfloat16)
    return (attn_grad, gain_part)


def to_heads(matrix, tile_count):
    return matrix.reshape(matrix.shape[0], tile_count, -1)


def from_heads(result, tile_count, rows_here):
    return result.reshape(tile_count, rows_here, -1)


def attend(head_q, head_k, head_v, head_g, valid_keys):
    patches, heads_here, head_size = head_q.shape
    block = min(512, patches)
    factor = head_size ** (-0.5)
    key_live = jnp.arange(patches) < valid_keys

    def one_block(index, carried):
        grad_q, grad_k, grad_v = carried
        start = index * block
        query_block = lax.dynamic_slice_in_dim(head_q, start, block, 0)
        grads_block = lax.dynamic_slice_in_dim(head_g, start, block, 0)
        scores = (
            jnp.einsum("bhe,khe->hbk", query_block, head_k, preferred_element_type=jnp.float32)
            * factor
        )
        scores = jnp.where(key_live[None, None, :], scores, -1e30)
        largest = jnp.max(scores, axis=-1, keepdims=True)
        expons = jnp.exp(scores - largest)
        probs = expons / jnp.sum(expons, axis=-1, keepdims=True)
        low_probs = probs.astype(jnp.bfloat16)
        grad_v = grad_v + jnp.einsum(
            "hbk,bhe->khe", low_probs, grads_block, preferred_element_type=jnp.float32
        )
        dprobs = jnp.einsum("bhe,khe->hbk", grads_block, head_v, preferred_element_type=jnp.float32)
        spread = jnp.sum(probs * dprobs, axis=-1, keepdims=True)
        dscores = (probs * (dprobs - spread)).astype(jnp.bfloat16)
        block_grad = (
            jnp.einsum("hbk,khe->bhe", dscores, head_k, preferred_element_type=jnp.float32) * factor
        )
        grad_k = grad_k + jnp.einsum(
            "hbk,bhe->khe", dscores, query_block, preferred_element_type=jnp.float32
        )
        grad_q = lax.dynamic_update_slice_in_dim(grad_q, block_grad.astype(jnp.bfloat16), start, 0)
        return (grad_q, grad_k, grad_v)

    initial = (
        jnp.zeros(head_q.shape, jnp.bfloat16),
        jnp.zeros(head_q.shape, jnp.float32),
        jnp.zeros(head_q.shape, jnp.float32),
    )
    upper = (valid_keys + block - 1) // block
    grad_q, grad_k, grad_v = lax.fori_loop(0, upper, one_block, initial)
    return (grad_q, (grad_k * factor).astype(jnp.bfloat16), grad_v.astype(jnp.bfloat16))


def body(query, keys, values, out_weight, hidden, gain, seq_grad, splice_at, merged_count):
    tile_count = lax.axis_size(TILE)
    width = query.shape[-1]
    rows_here = query.shape[1]
    whole_weight = lax.all_gather(out_weight, TILE, axis=0, tiled=True)
    patch_grad = splice_back(seq_grad, splice_at, merged_count, width)
    attn_grad, gain_part = norm_backward(hidden, gain, patch_grad)
    core_grad = jnp.einsum(
        "pd,cd->pc", attn_grad, whole_weight, preferred_element_type=jnp.float32
    ).astype(jnp.bfloat16)
    head_q, head_k, head_v, head_g = sent_together(
        (
            to_heads(query[0], tile_count),
            to_heads(keys[0], tile_count),
            to_heads(values[0], tile_count),
            to_heads(core_grad, tile_count),
        ),
        TILE,
        1,
        0,
        2,
    )
    gain_grad = by_axis(gain_part, IMG_TILE)
    valid_keys = 4 * merged_count[0]
    grad_q, grad_k, grad_v = attend(head_q, head_k, head_v, head_g, valid_keys)
    back_q, back_k, back_v = sent_together(
        (
            from_heads(grad_q, tile_count, rows_here),
            from_heads(grad_k, tile_count, rows_here),
            from_heads(grad_v, tile_count, rows_here),
        ),
        TILE,
        0,
        2,
        1,
    )
    return (back_q, back_k, back_v, gain_grad)


def solution(mesh):
    finer = Mesh(mesh.devices.reshape(8, 8, 8, 2), ("img_0", "img_1", "tile_0", "tile_1"))
    return jax.shard_map(
        body,
        mesh=finer,
        in_specs=(
            P(IMG, TILE, None),
            P(IMG, TILE, None),
            P(IMG, TILE, None),
            P(TILE, None),
            P(IMG, TILE, None),
            P(),
            P(IMG, TILE, None),
            P(IMG, TILE),
            P(IMG),
        ),
        out_specs=(P(IMG, TILE, None), P(IMG, TILE, None), P(IMG, TILE, None), P()),
        check_vma=False,
    )
```

profile of v0, /device:TPU:1, one launch (start us, length us, event | category | flops | bytes accessed | tf_op | source)
XLA Modules:
  0.0 230.9 jit_solution(4632674227943969175)
XLA Ops:
  10.3 23.6 %all_to_all.50 = s32[16,1,4]{2,1,0:T(1,128)S(1)} all-to-all(s32[16,1,4]{2,1,0:T(1,128)S(1)} %bitcast.173), channel_id=1, replica_groups=mesh['img_0'=8,'img_1'=8,'tile_0'=8,'tile_1'=2] {'tile_0','tile_1'}, dimensions={0} | all-to-all | bytes 512 | tf_op jit(solution)/shard_map/all_to_all | solution.py:52
  35.6 1.3 select_select_fusion
  37.0 4.2 %all-to-all-start.1 = ((bf16[16,4,5120]{2,1,0:T(4,128)(2,1)}), bf16[16,4,5120]{2,1,0:T(4,128)(2,1)S(1)}, u32[]{:S(2)}, u32[]{:S(2)}) async-start(bf16[16,4,5120]{2,1,0:T(4,128)(2,1)} %select_select_fusion), calls=%async_computation.1 | async-start | bytes 1310720 | tf_op jit(solution)/shard_map/all_to_all | solution.py:57
  43.4 1.9 copy.70
  45.5 21.6 %all-to-all-done.1 = bf16[16,4,5120]{2,1,0:T(4,128)(2,1)S(1)} async-done(((bf16[16,4,5120]{2,1,0:T(4,128)(2,1)}), bf16[16,4,5120]{2,1,0:T(4,128)(2,1)S(1)}, u32[]{:S(2)}, u32[]{:S(2)}) %all-to-all-start.1) | async-done | bytes 655392 | tf_op jit(solution)/shard_map/all_to_all | solution.py:57
  68.2 1.3 fusion.36
  69.6 9.2 %all-gather.2.cloned.1.call-done = bf16[1280,1280]{1,0:T(8,128)(2,1)} async-done(((bf16[80,1280]{1,0:T(8,128)(2,1)}), bf16[1280,1280]{1,0:T(8,128)(2,1)}) %all-gather.2.cloned.1.call-update) | async-done | bytes 3276816 | tf_op jit(solution)/shard_map/all_gather | solution.py:134
  78.8 3.2 %convolution_convert_fusion = bf16[128,1280]{1,0:T(8,128)(2,1)S(1)} fusion(bf16[1280,1280]{1,0:T(8,128)(2,1)} %all-gather.2.cloned.1.call-done, bf16[1,128,1280]{2,1,0:T(8,128)(2,1)} %param.15, f32[128]{0:T(128)S(1)} %broadcast_multiply_fusion, f32[1280]{0:T(1024)S(1)} %copy-done.6, f32[128]{0:T(128)S(1)} %add_rsqrt_fusion, ...), kind=kOutput, calls=%fused_computation.38 | convolution fusion | flops 421068800 | bytes 4266112 | tf_op jit(solution)/shard_map/pd,cd->pc/dot_general | solution.py:137
  83.4 5.2 %all-to-all-start.2 = ((bf16[128,16,320]{0,2,1:T(8,128)(2,1)}), bf16[128,16,320]{0,2,1:T(8,128)(2,1)S(1)}, u32[]{:S(2)}, u32[]{:S(2)}) async-start(bf16[128,16,320]{0,2,1:T(8,128)(2,1)} %pad_maximum_fusion), calls=%async_computation.2 | async-start | bytes 2621440 | tf_op jit(solution)/shard_map/all_to_all | solution.py:23
  88.6 33.3 %all-to-all-done.2 = bf16[128,16,320]{0,2,1:T(8,128)(2,1)S(1)} async-done(((bf16[128,16,320]{0,2,1:T(8,128)(2,1)}), bf16[128,16,320]{0,2,1:T(8,128)(2,1)S(1)}, u32[]{:S(2)}, u32[]{:S(2)}) %all-to-all-start.2) | async-done | bytes 1310752 | tf_op jit(solution)/shard_map/all_to_all | solution.py:23
  123.9 33.0 %while.15 = (s32[]{:T(128)}, bf16[2048,1,80]{0,2,1:T(8,128)(2,1)}, f32[2048,1,80]{0,2,1:T(8,128)S(1)}, f32[2048,1,80]{0,2,1:T(8,128)S(1)}, s32[]{:T(128)}, /*ind...) while((s32[]{:T(128)}, bf16[2048,1,80]{0,2,1:T(8,128)(2,1)}, ...), condition=%wide.region_9.10_spmd.clone, body=%wide.region_5.9_spmd.clone.sunk | while | flops 865485312 | bytes 42322180 | solution.py:126
  125.8 1.3 fusion.75
  127.1 1.5 multiply_reduce_fusion.2
  128.6 1.6 multiply_convert_fusion.3
  130.2 1.4 fusion.73
  134.1 1.3 fusion.75
  135.3 1.5 multiply_reduce_fusion.2
  136.8 1.6 multiply_convert_fusion.3
  138.4 1.4 fusion.73
  142.3 1.3 fusion.75
  143.6 1.5 multiply_reduce_fusion.2
  145.1 1.6 multiply_convert_fusion.3
  146.7 1.4 fusion.73
  150.5 1.3 fusion.75
  151.8 1.5 multiply_reduce_fusion.2
  153.3 1.6 multiply_convert_fusion.3
  154.9 1.4 fusion.73
  159.5 3.8 %all-to-all-start.3 = ((bf16[16,384,80]{1,2,0:T(8,128)(2,1)}), bf16[16,384,80]{1,2,0:T(8,128)(2,1)S(1)}, u32[]{:S(2)}, u32[]{:S(2)}) async-start(bf16[16,384,80]{1,2,0:T(8,128)(2,1)} %copy.79), calls=%async_computation.3 | async-start | bytes 1966080 | tf_op jit(solution)/shard_map/all_to_all | solution.py:23
  163.3 11.9 %psum.28 = f32[1280]{0:T(1024)S(1)} all-reduce(f32[1280]{0:T(1024)S(1)} %get-tuple-element.102), channel_id=1, replica_groups=mesh['img_0'=8,'img_1'=8,'tile_0'=8,'tile_1'=2] {'img_0'}, use_global_device_ids=true, to_apply=%region_11.12 | all-reduce | flops 1280 | bytes 10240 | tf_op jit(solution)/shard_map/psum | solution.py:32
  175.2 18.4 %psum.29 = f32[1280]{0:T(1024)S(1)} all-reduce(f32[1280]{0:T(1024)S(1)} %psum.28), channel_id=1, replica_groups=mesh['img_0'=8,'img_1'=8,'tile_0'=8,'tile_1'=2] {'img_1'}, use_global_device_ids=true, to_apply=%region_12.13 | all-reduce | flops 1280 | bytes 10240 | tf_op jit(solution)/shard_map/psum | solution.py:32
  193.5 13.8 %psum.30 = f32[1280]{0:T(1024)S(1)} all-reduce(f32[1280]{0:T(1024)S(1)} %psum.29), channel_id=1, replica_groups=mesh['img_0'=8,'img_1'=8,'tile_0'=8,'tile_1'=2] {'tile_0'}, use_global_device_ids=true, to_apply=%region_13.14 | all-reduce | flops 1280 | bytes 10240 | tf_op jit(solution)/shard_map/psum | solution.py:32
  207.3 13.8 %psum.31 = f32[1280]{0:T(1024)} all-reduce(f32[1280]{0:T(1024)S(1)} %psum.30), channel_id=1, replica_groups=mesh['img_0'=8,'img_1'=8,'tile_0'=8,'tile_1'=2] {'tile_1'}, use_global_device_ids=true, to_apply=%region_14.15 | all-reduce | flops 1280 | bytes 10240 | tf_op jit(solution)/shard_map/psum | solution.py:32
  (92 shorter events, 26.2 us)
Async XLA Ops:
  7.2 27.3 %copy-start = (bf16[1,128,5120]{2,1,0:T(8,128)(2,1)S(1)}, bf16[1,128,5120]{2,1,0:T(8,128)(2,1)}, u32[]{:S(2)}) copy-start(bf16[1,128,5120]{2,1,0:T(8,128)(2,1)} %param.17) | copy-start | bytes 3932164
  7.2 71.6 %all-gather.2.cloned.1.call-start = ((), (), s32[]{:S(2)}) async-start(), calls=%async_computation.4 | async-start | bytes 3481600 | tf_op jit(solution)/shard_map/all_gather | solution.py:134
  34.4 7.6 %copy-start.5 = (bf16[1,128,1280]{2,1,0:T(8,128)(2,1)S(1)}, bf16[1,128,1280]{2,1,0:T(8,128)(2,1)}, u32[]{:S(2)}) copy-start(bf16[1,128,1280]{2,1,0:T(8,128)(2,1)} %param.11) | copy-start | bytes 983044
  35.4 9.9 %copy-start.2 = (bf16[1,128,1280]{2,1,0:T(8,128)(2,1)S(1)}, bf16[1,128,1280]{2,1,0:T(8,128)(2,1)}, u32[]{:S(2)}) copy-start(bf16[1,128,1280]{2,1,0:T(8,128)(2,1)} %param.15) | copy-start | bytes 983044
  37.0 31.3 %copy-start.6 = (f32[1280]{0:T(1024)S(1)}, f32[1280]{0:T(1024)}, u32[]{:S(2)}) copy-start(f32[1280]{0:T(1024)} %param.16) | copy-start | bytes 15364
  37.0 30.1 %all-to-all-start.1 = ((bf16[16,4,5120]{2,1,0:T(4,128)(2,1)}), bf16[16,4,5120]{2,1,0:T(4,128)(2,1)S(1)}, u32[]{:S(2)}, u32[]{:S(2)}) async-start(bf16[16,4,5120]{2,1,0:T(4,128)(2,1)} %select_select_fusion), calls=%async_computation.1 | async-start | bytes 1310720 | tf_op jit(solution)/shard_map/all_to_all | solution.py:57
  67.3 15.0 %copy-start.1 = (bf16[1,128,1280]{1,2,0:T(8,128)(2,1)S(1)}, bf16[1,128,1280]{1,2,0:T(8,128)(2,1)}, u32[]{:S(2)}) copy-start(bf16[1,128,1280]{1,2,0:T(8,128)(2,1)} %copy.70) | copy-start | bytes 983044
  83.4 38.4 %all-to-all-start.2 = ((bf16[128,16,320]{0,2,1:T(8,128)(2,1)}), bf16[128,16,320]{0,2,1:T(8,128)(2,1)S(1)}, u32[]{:S(2)}, u32[]{:S(2)}) async-start(bf16[128,16,320]{0,2,1:T(8,128)(2,1)} %pad_maximum_fusion), calls=%async_computation.2 | async-start | bytes 2621440 | tf_op jit(solution)/shard_map/all_to_all | solution.py:23
  123.9 1.9 copy-start.4
  125.8 1.3 copy-start.3
  132.2 1.9 copy-start.4
  134.0 1.3 copy-start.3
  140.4 1.9 copy-start.4
  142.3 1.3 copy-start.3
  148.7 1.9 copy-start.4
  150.5 1.3 copy-start.3
  159.5 61.7 %all-to-all-start.3 = ((bf16[16,384,80]{1,2,0:T(8,128)(2,1)}), bf16[16,384,80]{1,2,0:T(8,128)(2,1)S(1)}, u32[]{:S(2)}, u32[]{:S(2)}) async-start(bf16[16,384,80]{1,2,0:T(8,128)(2,1)} %copy.79), calls=%async_computation.3 | async-start | bytes 1966080 | tf_op jit(solution)/shard_map/all_to_all | solution.py:23
Sparse Core Ops, SparseCore 0:
  10.7 68.0 all-gather.1
where the time goes:
time: 231 us
  blocking collectives  81.5 us (35%)
  waiting for transfers between devices  64.8 us (28%)
  matrix products  25.8 us (11%)
  other arithmetic  16 us (7%)
  between operations  14.9 us (6%)
  local copies, waits for them, and re-layouts  14.4 us (6%)
  starting transfers between devices  13.2 us (6%)
    psum x4, blocking collectives, by_axis(): x = lax.psum(x, axis)  57.9 us
    all_to_all x2, waiting for transfers between devices, sent_together(): lax.all_to_all(both, axis, split_axis=split_dim, concat_axis=concat_dim,...  33.3 us
    all_to_all x1, blocking collectives, splice_back(): lax.all_to_all(requests, TILE, split_axis=0, concat_axis=0, tiled=True)  23.6 us
    all_to_all x1, waiting for transfers between devices, splice_back(): lax.all_to_all(found_rows, TILE, split_axis=0, concat_axis=0, tiled=True)  21.6 us
    all_gather x1, waiting for transfers between devices, body(): whole_weight = lax.all_gather(out_weight, TILE, axis=0, tiled=True)  9.23 us
    all_to_all x2, starting transfers between devices, sent_together(): lax.all_to_all(both, axis, split_axis=split_dim, concat_axis=concat_dim,...  8.94 us
    unnamed x19, local copies, waits for them, and re-layouts  7.15 us
    convert_element_type x4, other arithmetic, one_block(): dscores = (probs * (dprobs - spread)).astype(jnp.bfloat16)  6.2 us
  transfers between devices with their start and end apart: 4, of which 3 were waited for; matrix products, arithmetic and copies ran while one was open for 5% of the time, Pallas kernels for 0%

commit v1 on v0

v1 whole, which is shorter than its diff:
```python
import math

import jax
import jax.numpy as jnp
from jax import lax
from jax.experimental import pallas as pl
from jax.experimental.pallas import tpu as pltpu
from jax.sharding import PartitionSpec as P

MESH = pl.DeviceIdType.MESH
F32 = jnp.float32
BF16 = jnp.bfloat16

NORM_EPS = 1e-06
HEAD = 80
D = 1280
T = 16
ROWS = 128
PATCHES = 2048
HALF = 640
QB = 256
FACTOR = HEAD ** (-0.5)
REQ, W1, W2, W3, ROW, Q, K, V, G, DQ, DK, DV, GA, GB, GC = range(15)


def dot(a, b, ca, cb):
    return lax.dot_general(a, b, (((ca,), (cb,)), ((), ())), preferred_element_type=F32)


def kernel(
    pos_ref, count_ref, q_ref, k_ref, v_ref, w_ref, h_ref, gain_ref, seq_ref,
    oq_ref, ok_ref, ov_ref, og_ref,
    qs, ks, vs, gs, qt, kt, vt, gt, wall, reqs, reqr, reqt, rsend, rrecv,
    probs, dv, dk, dqb, dkb, dvb, bq, bk, bv,
    g1s, g1, g2s, g2, g3s, g3, ssem, rsem,
):
    img = lax.axis_index("img")
    tile = lax.axis_index("tile")
    x, z = img // 8, img % 8
    y, c = tile // 2, tile % 2
    u = x * (1 - c) + z * c
    sigma = u % 4
    me80 = pl.multiple_of(tile * HEAD, 16)
    me128 = pl.multiple_of(tile * ROWS, ROWS)

    def peer(delta):
        return (tile + delta) % T

    def along(d):
        return ((x + (1 - c) * d) % 8) * 8 + (z + c * d) % 8

    def on_x(d):
        return ((x + d) % 8) * 8 + z

    def on_z(d):
        return x * 8 + (z + d) % 8

    def link(src, dst, kind, to_img, to_tile):
        return pltpu.make_async_remote_copy(
            src_ref=src,
            dst_ref=dst,
            send_sem=ssem.at[kind],
            recv_sem=rsem.at[kind],
            device_id=(to_img, to_tile),
            device_id_type=MESH,
        )

    def arrived(ref, kind):
        link(ref, ref, kind, img, peer(1)).wait_recv()

    def sent(ref, kind):
        link(ref, ref, kind, img, peer(1)).wait_send()

    def to_tiles(fn):
        def step(delta, carry):
            fn(peer(delta))
            return carry

        lax.fori_loop(1, T, step, 0)

    barrier = pltpu.get_barrier_semaphore()

    def hello(to_img, to_tile):
        pl.semaphore_signal(barrier, inc=1, device_id=(to_img, to_tile), device_id_type=MESH)

    def hello_plane(delta, carry):
        hello(on_x(delta), tile)
        hello(on_z(delta), tile)
        return carry

    to_tiles(lambda t: hello(img, t))
    lax.fori_loop(1, 8, hello_plane, 0)

    count = count_ref[0]
    lane = lax.broadcasted_iota(jnp.int32, (8, 128), 1)
    span = lax.broadcasted_iota(jnp.int32, (8, 128), 0) * 4 + lane // 32
    slot = lane % 4
    part = (lane % 32) // 4
    seen = jnp.zeros((8, 128), jnp.int32)
    want = jnp.full((8, 128), -1, jnp.int32)
    whose = jnp.full((8, 128), -1, jnp.int32)
    for r in range(32):
        at = pos_ref[0, r]
        live = jnp.where(tile * 32 + r < count, at // 128, -1)
        take = (span == live) & (seen == slot)
        want = jnp.where(take, at % 128, want)
        whose = jnp.where(take, r, whose)
        seen = seen + jnp.where(span == live, 1, 0)
    for o in range(4):
        reqs[o] = want[o : o + 1]

    for src, mid, dst in ((q_ref, qs, qt), (k_ref, ks, kt), (v_ref, vs, vt)):
        for b in range(10):
            mid[b * 128 : (b + 1) * 128, :] = src[:, b * 128 : (b + 1) * 128].T
        dst[0:HEAD, pl.ds(me128, ROWS)] = mid[pl.ds(me80, HEAD), :]
    row0 = lax.broadcasted_iota(jnp.int32, (48, PATCHES), 0) == 0
    key_at = lax.broadcasted_iota(jnp.int32, (48, PATCHES), 1)
    qt[HEAD:128, :] = jnp.where(row0, 1.0, 0.0).astype(BF16)
    kt[HEAD:128, :] = jnp.where(row0 & (key_at >= 4 * count), -1e30, 0.0).astype(BF16)
    vt[HEAD:128, :] = jnp.zeros((48, PATCHES), BF16)
    gt[HEAD:128, :] = jnp.zeros((48, PATCHES), BF16)
    dv[...] = jnp.zeros_like(dv)
    dk[...] = jnp.zeros_like(dk)
    reqr[pl.ds(tile, 1)] = reqs[pl.ds(tile // 4, 1)]
    w_rows = pl.ds(pl.multiple_of((sigma // 2) * 32, 32), 48)
    w_cols = pl.ds(pl.multiple_of((sigma % 2) * HALF, 128), HALF)
    wall[c, sigma, y] = w_ref[w_rows, w_cols]

    pl.semaphore_wait(barrier, T - 1 + 14)

    to_tiles(lambda t: link(reqs.at[t // 4], reqr.at[tile], REQ, img, t).start())

    def send_w1(delta, carry):
        link(w_ref.at[w_rows, w_cols], wall.at[c, sigma, y], W1, img, (tile + 2 * delta) % T).start()
        return carry

    lax.fori_loop(1, 8, send_w1, 0)

    arrived(reqr.at[0 : T - 1], REQ)
    asked = reqr[...].reshape(T, 128).astype(F32)
    reqt[...] = jnp.concatenate([asked, jnp.full((112, 128), -1.0, F32)], axis=0).T
    mine = reqt[pl.ds(pl.multiple_of((tile % 4) * 32, 32), 32), :].astype(jnp.int32)
    wide = lax.broadcasted_iota(jnp.int32, (32, 128), 1)
    row_part = lax.broadcasted_iota(jnp.int32, (32, 128), 0) // 4
    for d in range(0, T, 4):
        hits = [jnp.broadcast_to(mine[:, e : e + 1], (32, 128)) == wide for e in range(d, d + 4)]
        rows = jnp.zeros((128, HALF), F32)
        for s in range(8):
            pick = jnp.concatenate(
                [jnp.where(hit & (row_part == s), 1.0, 0.0) for hit in hits], axis=0
            ).astype(BF16)
            rows = rows + dot(pick, seq_ref[:, s * HALF : (s + 1) * HALF], 1, 0)
        rsend[d : d + 4] = rows.astype(BF16).reshape(4, 32, HALF)
    rrecv[pl.ds(tile, 1)] = rsend[pl.ds(tile, 1)]
    to_tiles(lambda t: link(rsend.at[t], rrecv.at[tile], ROW, img, t).start())

    def block_of(ref, t):
        return ref.at[pl.ds(pl.multiple_of(t * HEAD, 16), HEAD), :]

    def head_rows(ref):
        return ref.at[0:HEAD, pl.ds(me128, ROWS)]

    to_tiles(lambda t: link(block_of(qs, t), head_rows(qt), Q, img, t).start())
    to_tiles(lambda t: link(block_of(ks, t), head_rows(kt), K, img, t).start())
    to_tiles(lambda t: link(block_of(vs, t), head_rows(vt), V, img, t).start())

    own = wall.at[c, sigma]
    lower, upper = wall.at[c, sigma, 0:4], wall.at[c, sigma, 4:8]
    other = tile + 1 - 2 * c
    arrived(wall.at[0, 0, 0:7], W1)
    link(own, own, W2, along(1), tile).start()
    link(own, own, W2, along(7), tile).start()
    link(lower, lower, W2, along(2), tile).start()
    link(upper, upper, W2, along(6), tile).start()
    link(own, own, W3, img, other).start()
    arrived(wall.at[0, 0:3], W2)
    for i in range(1, 4):
        more = wall.at[c, (sigma + i) % 4]
        link(more, more, W3, img, other).start()

    hidden = h_ref[...].astype(F32)
    inverse = lax.rsqrt(jnp.mean(hidden * hidden, axis=1, keepdims=True) + NORM_EPS)
    normed = hidden * inverse
    wide_rows = lax.broadcasted_iota(jnp.int32, (ROWS, 128), 0)
    lane_part = (lax.broadcasted_iota(jnp.int32, (ROWS, 128), 1) % 32) // 4
    arrived(rrecv.at[0 : T - 1], ROW)
    halves = []
    for h in range(2):
        total = jnp.zeros((ROWS, HALF), F32)
        for o in range(4):
            owner = jnp.broadcast_to(whose[o : o + 1], (ROWS, 128))
            pick = (owner == wide_rows // 4) & (lane_part == 2 * (wide_rows % 4) + h)
            total = total + dot(
                jnp.where(pick, 1.0, 0.0).astype(BF16),
                rrecv[4 * o : 4 * o + 4].reshape(128, HALF),
                1,
                0,
            )
        halves.append(total)
    upstream = jnp.concatenate(halves, axis=1)
    both = upstream * normed
    part_sum = jnp.sum(both, axis=0, keepdims=True)
    gain = gain_ref[...]
    mean = jnp.mean(gain * both, axis=1, keepdims=True)
    attn = (inverse * (gain * upstream - normed * mean)).astype(BF16)
    g1s[...] = part_sum
    g1[pl.ds(tile, 1)] = part_sum.reshape(1, 1, D)

    arrived(wall.at[0], W3)
    for c2 in range(2):
        for ch in range(2):
            acc = jnp.zeros((384, ROWS), F32)
            for dh in range(2):
                acc = acc + dot(
                    wall[c2, ch * 2 + dh].reshape(384, HALF), attn[:, dh * HALF : (dh + 1) * HALF], 1, 1
                )
            acc = acc.astype(BF16)
            for y2 in range(8):
                base = (2 * y2 + c2) * HEAD
                if ch == 0:
                    gs[base : base + 48, :] = acc[48 * y2 : 48 * y2 + 48]
                else:
                    gs[base + 48 : base + 80, :] = acc[48 * y2 + 16 : 48 * y2 + 48]
    gt[0:HEAD, pl.ds(me128, ROWS)] = gs[pl.ds(me80, HEAD), :]
    to_tiles(lambda t: link(g1s, g1.at[tile], GA, img, t).start())
    to_tiles(lambda t: link(block_of(gs, t), head_rows(gt), G, img, t).start())

    arrived(qt.at[0:HEAD, 0 : PATCHES - ROWS], Q)
    arrived(kt.at[0:HEAD, 0 : PATCHES - ROWS], K)
    rate = FACTOR * math.log2(math.e)

    def soften(j, carry):
        at = pl.ds(pl.multiple_of(j * QB, QB), QB)
        scores = dot(qt[:, at].T, kt[...], 1, 0)
        largest = jnp.max(scores, axis=1, keepdims=True)
        expons = jnp.exp2((scores - largest) * rate)
        probs[at, :] = (expons * (1.0 / jnp.sum(expons, axis=1, keepdims=True))).astype(BF16)
        return carry

    lax.fori_loop(0, PATCHES // QB, soften, 0)

    arrived(g1.at[0 : T - 1], GA)
    total = g1[0]
    for i in range(1, T):
        total = total + g1[i]
    g2s[...] = total
    g2[pl.ds(x, 1)] = total.reshape(1, 1, D)

    arrived(vt.at[0:HEAD, 0 : PATCHES - ROWS], V)

    def send_g2(delta, carry):
        link(g2s, g2.at[x], GB, on_x(delta), tile).start()
        return carry

    lax.fori_loop(1, 8, send_g2, 0)
    arrived(gt.at[0:HEAD, 0 : PATCHES - ROWS], G)

    def backward(j, carry):
        at = pl.ds(pl.multiple_of(j * QB, QB), QB)
        grads = gt[:, at]
        dprobs = dot(grads.T, vt[...], 1, 0)
        low = probs[at, :]
        weight = low.astype(F32)
        prod = weight * dprobs
        spread = jnp.sum(prod, axis=1, keepdims=True)
        dscores = (prod - weight * spread).astype(BF16)
        dv[...] += dot(grads[0:HEAD], low, 1, 0)
        dk[...] += dot(qt[0:HEAD, at], dscores, 1, 0)
        dq = dot(kt[0:HEAD, :], dscores, 1, 1)
        dqb[:, at] = (dq * FACTOR).astype(BF16)
        return carry

    lax.fori_loop(0, PATCHES // QB, backward, 0)

    def columns(ref, t):
        return ref.at[:, pl.ds(pl.multiple_of(t * ROWS, ROWS), ROWS)]

    def back(src, dst, kind):
        dst[pl.ds(me80, HEAD), :] = src[:, pl.ds(me128, ROWS)]
        to_tiles(lambda t: link(columns(src, t), block_of(dst, tile), kind, img, t).start())

    dvb[...] = dv[...].astype(BF16)
    dkb[...] = (dk[...] * FACTOR).astype(BF16)
    back(dqb, bq, DQ)
    back(dvb, bv, DV)
    back(dkb, bk, DK)

    arrived(g2.at[0:7], GB)
    total = g2[0]
    for i in range(1, 8):
        total = total + g2[i]
    g3s[...] = total
    g3[pl.ds(z, 1)] = total.reshape(1, 1, D)

    def send_g3(delta, carry):
        link(g3s, g3.at[z], GC, on_z(delta), tile).start()
        return carry

    lax.fori_loop(1, 8, send_g3, 0)
    arrived(g3.at[0:7], GC)
    total = g3[0]
    for i in range(1, 8):
        total = total + g3[i]
    og_ref[...] = total

    for src, dst, kind in ((bq, oq_ref, DQ), (bv, ov_ref, DV), (bk, ok_ref, DK)):
        arrived(src.at[0 : D - HEAD], kind)
        for b in range(10):
            dst[:, b * 128 : (b + 1) * 128] = src[b * 128 : (b + 1) * 128, :].T

    sent(reqr.at[0 : T - 1], REQ)
    sent(wall.at[0, 0, 0:7], W1)
    sent(wall.at[0, 0:3], W2)
    sent(wall.at[0], W3)
    sent(rsend.at[0 : T - 1], ROW)
    for kind in (Q, K, V, G, DQ, DK, DV):
        sent(qs.at[0 : D - HEAD], kind)
    sent(g1.at[0 : T - 1], GA)
    sent(g2.at[0:7], GB)
    sent(g3.at[0:7], GC)


def body(query, keys, values, out_weight, hidden, gain, seq_grad, splice_at, merged_count):
    smem = pl.BlockSpec(memory_space=pltpu.SMEM)
    vmem = pl.BlockSpec(memory_space=pltpu.VMEM)
    block = jax.ShapeDtypeStruct((ROWS, D), BF16)
    head = pltpu.VMEM((128, PATCHES), BF16)
    blocks = pltpu.VMEM((D, ROWS), BF16)
    grads = pl.pallas_call(
        kernel,
        out_shape=(block, block, block, jax.ShapeDtypeStruct((1, D), F32)),
        in_specs=[smem, smem] + [vmem] * 7,
        out_specs=(vmem,) * 4,
        scratch_shapes=[
            *[blocks] * 4,
            *[head] * 4,
            pltpu.VMEM((2, 4, 8, 48, HALF), BF16),
            pltpu.VMEM((4, 1, 128), jnp.int32),
            pltpu.VMEM((T, 1, 128), jnp.int32),
            pltpu.VMEM((128, 128), F32),
            pltpu.VMEM((T, 32, HALF), BF16),
            pltpu.VMEM((T, 32, HALF), BF16),
            pltpu.VMEM((PATCHES, PATCHES), BF16),
            pltpu.VMEM((HEAD, PATCHES), F32),
            pltpu.VMEM((HEAD, PATCHES), F32),
            *[pltpu.VMEM((HEAD, PATCHES), BF16)] * 3,
            *[blocks] * 3,
            pltpu.VMEM((1, D), F32),
            pltpu.VMEM((T, 1, D), F32),
            pltpu.VMEM((1, D), F32),
            pltpu.VMEM((8, 1, D), F32),
            pltpu.VMEM((1, D), F32),
            pltpu.VMEM((8, 1, D), F32),
            pltpu.SemaphoreType.DMA((15,)),
            pltpu.SemaphoreType.DMA((15,)),
        ],
        compiler_params=pltpu.CompilerParams(
            collective_id=0, has_side_effects=True, vmem_limit_bytes=60 * 1024 * 1024
        ),
    )(
        splice_at,
        merged_count,
        query[0],
        keys[0],
        values[0],
        out_weight,
        hidden[0],
        gain[None, :],
        seq_grad[0],
    )
    return grads[0][None], grads[1][None], grads[2][None], grads[3][0]


def solution(mesh):
    rows = P("img", "tile", None)
    return jax.shard_map(
        body,
        mesh=mesh,
        in_specs=(rows, rows, rows, P("tile", None), rows, P(), rows, P("img", "tile"), P("img")),
        out_specs=(rows, rows, rows, P()),
        check_vma=False,
    )
```

time: 231 us -> 126 us (0.55)
  Pallas kernels: 0 us -> 118 us
  blocking collectives: 81.5 us -> 0 us
  waiting for transfers between devices: 64.8 us -> 0 us
  matrix products: 25.8 us -> 0 us
  other arithmetic: 16 us -> 1.35 us
  between operations: 14.9 us -> 1.3 us
  starting transfers between devices: 13.2 us -> 0 us
  local copies, waits for them, and re-layouts: 14.4 us -> 5.46 us
    pallas_call x0 -> x1, Pallas kernels: none -> 118 us  [body(): pl.pallas_call(kernel, out_shape=(block, block, block, jax.ShapeDtypeStru...]
    psum x4 -> x0, blocking collectives: 57.9 us -> none  [by_axis(): x = lax.psum(x, axis)]
    all_to_all x3 -> x0, waiting for transfers between devices: 54.9 us -> none  [the longest x2 33.3 us: sent_together(): lax.all_to_all(both, axis, split_axis=split_dim, concat_axis=concat_dim,...]
    dot_general x21 -> x0, matrix products: 25.8 us -> none  [the longest x4 6 us: one_block(): jnp.einsum('bhe,khe->hbk', grads_block, head_v, preferred_element_type=jn...]
    all_to_all x1 -> x0, blocking collectives: 23.6 us -> none  [splice_back(): lax.all_to_all(requests, TILE, split_axis=0, concat_axis=0, tiled=True)]
    all_to_all x3 -> x0, starting transfers between devices: 13.1 us -> none  [the longest x2 8.94 us: sent_together(): lax.all_to_all(both, axis, split_axis=split_dim, concat_axis=concat_dim,...]
    all_gather x1 -> x0, waiting for transfers between devices: 9.23 us -> none  [body(): whole_weight = lax.all_gather(out_weight, TILE, axis=0, tiled=True)]
    convert_element_type x5 -> x0, other arithmetic: 6.27 us -> none  [the longest x4 6.2 us: one_block(): dscores = (probs * (dprobs - spread)).astype(jnp.bfloat16)]
  transfers between devices with their start and end apart: 4 -> 0, of which waited for: 3 -> 0; matrix products, arithmetic and copies ran while one was open for 5% -> 0% of each run, Pallas kernels for 0% -> 0%
where the time goes in v1:
time: 126 us
  Pallas kernels  118 us (94%)
  local copies, waits for them, and re-layouts  5.46 us (4%)
  other arithmetic  1.35 us (1%)
  between operations  1.3 us (1%)
    pallas_call x1, Pallas kernels, body(): pl.pallas_call(kernel, out_shape=(block, block, block, jax.ShapeDtypeStru...  118 us
    unnamed x5, local copies, waits for them, and re-layouts  4.16 us

profile of v1, /device:TPU:1, one launch (start us, length us, event | category | flops | bytes accessed | tf_op | source)
XLA Modules:
  0.0 125.8 jit_solution(14361039389368181973)
XLA Ops:
  0.6 1.3 %broadcast_in_dim.12.gain_ref = f32[1,1280]{1,0:T(1,128)} reshape(f32[1280]{0:T(1024)} %param.14) | data formatting | bytes 10240 | tf_op jit(solution)/shard_map/broadcast_in_dim | solution.py:368
  2.6 117.7 %shard_map.120 = (bf16[128,1280]{1,0:T(8,128)(2,1)}, bf16[128,1280]{1,0:T(8,128)(2,1)}, bf16[128,1280]{1,0:T(8,128)(2,1)}, f32[1,1280]{1,0:T(1,128)}) custom-call(s32[1,32]{1,0:T(1,128)} %pos_ref.1, s32[1]{0:T(128)S(6)} %copy.16.count_ref, bf16[128,1280]{1,0:T(8,128)(2,1)} %bitcast.9, bf16[128,1280]{1,0:T(8,128)(2,1)} %bitcast.10, ...), custom_call_target="tpu_custom_call" | custom-call | tf_op jit(solution)/shard_map/pallas_call | solution.py:329
  120.3 0.0 copy-start
  120.3 1.4 %reduce = f32[1280]{0:T(1024)} reduce(f32[1,1280]{1,0:T(1,128)} %get-tuple-element.11, f32[]{:T(128)} %constant.7), dimensions={0}, to_apply=%get-tuple-element.11.reduce_sub_computation | reduce | bytes 10244 | tf_op jit(solution)/shard_map/pallas_call | solution.py:329
  121.7 1.7 %copy.17 = bf16[1,128,1280]{2,1,0:T(8,128)(2,1)} copy(bf16[1,128,1280]{2,1,0:T(8,128)(2,1)} %bitcast.15) | data formatting | bytes 655360
  123.4 1.7 %copy.18 = bf16[1,128,1280]{2,1,0:T(8,128)(2,1)} copy(bf16[1,128,1280]{2,1,0:T(8,128)(2,1)} %bitcast.14) | data formatting | bytes 655360
  125.1 0.0 copy-done
  125.1 0.7 copy.19
Async XLA Ops:
  120.3 4.8 %copy-start = (bf16[128,1280]{1,0:T(8,128)(2,1)S(1)}, bf16[128,1280]{1,0:T(8,128)(2,1)}, u32[]{:S(2)}) copy-start(bf16[128,1280]{1,0:T(8,128)(2,1)} %get-tuple-element.10) | copy-start | bytes 983044

commit v2 on v1

--- a/solution.py
+++ b/solution.py
@@ -20,7 +20,8 @@
 HALF = 640
 QB = 256
 FACTOR = HEAD ** (-0.5)
-REQ, W1, W2, W3, ROW, Q, K, V, G, DQ, DK, DV, GA, GB, GC = range(15)
+REQ, W1, W3, ROW, Q, K, V, DQ, DK, DV, GA, GB, GC, W2 = range(14)
+G = W2 + 8
 
 
 def dot(a, b, ca, cb):
@@ -28,18 +29,19 @@
 
 
 def kernel(
-    pos_ref, count_ref, q_ref, k_ref, v_ref, w_ref, h_ref, gain_ref, seq_ref,
-    oq_ref, ok_ref, ov_ref, og_ref,
+    pos_ref, count_ref, gain_ref, q_hbm, k_hbm, v_hbm, w_hbm, h_hbm, seq_hbm,
+    out_hbm, og_ref,
+    q_ref, k_ref, v_ref, w_ref, h_ref, seq_ref,
     qs, ks, vs, gs, qt, kt, vt, gt, wall, reqs, reqr, reqt, rsend, rrecv,
-    probs, dv, dk, dqb, dkb, dvb, bq, bk, bv,
-    g1s, g1, g2s, g2, g3s, g3, ssem, rsem,
+    probs, dk, dqb, dkb, dvb, bq, bk, bv,
+    g1s, g1, g2s, g2, g3s, g3, ssem, rsem, lsem,
 ):
     img = lax.axis_index("img")
     tile = lax.axis_index("tile")
     x, z = img // 8, img % 8
     y, c = tile // 2, tile % 2
     u = x * (1 - c) + z * c
-    sigma = u % 4
+    sigma = u // 2
     me80 = pl.multiple_of(tile * HEAD, 16)
     me128 = pl.multiple_of(tile * ROWS, ROWS)
 
@@ -91,7 +93,16 @@
     to_tiles(lambda t: hello(img, t))
     lax.fori_loop(1, 8, hello_plane, 0)
 
-    count = count_ref[0]
+    loads = [
+        pltpu.make_async_copy(src, dst, lsem.at[i])
+        for i, (src, dst) in enumerate(
+            ((q_hbm, q_ref), (k_hbm, k_ref), (v_hbm, v_ref), (w_hbm, w_ref), (seq_hbm, seq_ref), (h_hbm, h_ref))
+        )
+    ]
+    for load in loads:
+        load.start()
+
+    count = count_ref[...].reshape(1, 1)
     lane = lax.broadcasted_iota(jnp.int32, (8, 128), 1)
     span = lax.broadcasted_iota(jnp.int32, (8, 128), 0) * 4 + lane // 32
     slot = lane % 4
@@ -101,7 +112,7 @@
     whose = jnp.full((8, 128), -1, jnp.int32)
     for r in range(32):
         at = pos_ref[0, r]
-        live = jnp.where(tile * 32 + r < count, at // 128, -1)
+        live = jnp.where(jnp.broadcast_to(count, (8, 128)) > tile * 32 + r, at // 128, -1)
         take = (span == live) & (seen == slot)
         want = jnp.where(take, at % 128, want)
         whose = jnp.where(take, r, whose)
@@ -109,34 +120,42 @@
     for o in range(4):
         reqs[o] = want[o : o + 1]
 
-    for src, mid, dst in ((q_ref, qs, qt), (k_ref, ks, kt), (v_ref, vs, vt)):
-        for b in range(10):
-            mid[b * 128 : (b + 1) * 128, :] = src[:, b * 128 : (b + 1) * 128].T
-        dst[0:HEAD, pl.ds(me128, ROWS)] = mid[pl.ds(me80, HEAD), :]
     row0 = lax.broadcasted_iota(jnp.int32, (48, PATCHES), 0) == 0
     key_at = lax.broadcasted_iota(jnp.int32, (48, PATCHES), 1)
     qt[HEAD:128, :] = jnp.where(row0, 1.0, 0.0).astype(BF16)
-    kt[HEAD:128, :] = jnp.where(row0 & (key_at >= 4 * count), -1e30, 0.0).astype(BF16)
+    kt[HEAD:128, :] = jnp.where(row0 & (key_at >= jnp.broadcast_to(4 * count, (48, PATCHES))), -1e30, 0.0).astype(BF16)
     vt[HEAD:128, :] = jnp.zeros((48, PATCHES), BF16)
     gt[HEAD:128, :] = jnp.zeros((48, PATCHES), BF16)
-    dv[...] = jnp.zeros_like(dv)
     dk[...] = jnp.zeros_like(dk)
     reqr[pl.ds(tile, 1)] = reqs[pl.ds(tile // 4, 1)]
     w_rows = pl.ds(pl.multiple_of((sigma // 2) * 32, 32), 48)
     w_cols = pl.ds(pl.multiple_of((sigma % 2) * HALF, 128), HALF)
-    wall[c, sigma, y] = w_ref[w_rows, w_cols]
+    for i, (src, mid, dst) in enumerate(((q_ref, qs, qt), (k_ref, ks, kt), (v_ref, vs, vt))):
+        loads[i].wait()
+        for b in range(10):
+            mid[b * 128 : (b + 1) * 128, :] = src[:, b * 128 : (b + 1) * 128].T
+        dst[0:HEAD, pl.ds(me128, ROWS)] = mid[pl.ds(me80, HEAD), :]
+    loads[3].wait()
+    mine_too = (y + u) % 2 == 0
+
+    @pl.when(mine_too)
+    def _():
+        wall[c, u, y // 2] = w_ref[w_rows, w_cols]
 
     pl.semaphore_wait(barrier, T - 1 + 14)
 
     to_tiles(lambda t: link(reqs.at[t // 4], reqr.at[tile], REQ, img, t).start())
 
-    def send_w1(delta, carry):
-        link(w_ref.at[w_rows, w_cols], wall.at[c, sigma, y], W1, img, (tile + 2 * delta) % T).start()
-        return carry
-
-    lax.fori_loop(1, 8, send_w1, 0)
+    @pl.when(mine_too)
+    def _():
+        def send_w1(delta, carry):
+            link(w_ref.at[w_rows, w_cols], wall.at[c, u, y // 2], W1, img, (tile + 2 * delta) % T).start()
+            return carry
+
+        lax.fori_loop(1, 8, send_w1, 0)
 
     arrived(reqr.at[0 : T - 1], REQ)
+    loads[4].wait()
     asked = reqr[...].reshape(T, 128).astype(F32)
     reqt[...] = jnp.concatenate([asked, jnp.full((112, 128), -1.0, F32)], axis=0).T
     mine = reqt[pl.ds(pl.multiple_of((tile % 4) * 32, 32), 32), :].astype(jnp.int32)
@@ -160,24 +179,41 @@
     def head_rows(ref):
         return ref.at[0:HEAD, pl.ds(me128, ROWS)]
 
+    other = tile + 1 - 2 * c
+
+    @pl.when(mine_too)
+    def _():
+        arrived(wall.at[0, 0, 0:3], W1)
+
+    @pl.when((y + u) % 2 == 1)
+    def _():
+        arrived(wall.at[0, 0], W1)
+
+    own = wall.at[c, u]
+    link(own, own, W2 + 1, along(1), tile).start()
+    link(own, own, W2 + 7, along(7), tile).start()
+    link(own, own, W3, img, other).start()
+
     to_tiles(lambda t: link(block_of(qs, t), head_rows(qt), Q, img, t).start())
+
+    def pass_on(d):
+        arrived(wall.at[0, 0], W2 + d)
+        more = wall.at[c, (u - d + 8) % 8]
+        if d in (1, 2, 3):
+            link(more, more, W2 + d + 1, along(1), tile).start()
+        if d in (7, 6):
+            link(more, more, W2 + d - 1, along(7), tile).start()
+        link(more, more, W3, img, other).start()
+
+    for d in (1, 7, 2, 6):
+        pass_on(d)
     to_tiles(lambda t: link(block_of(ks, t), head_rows(kt), K, img, t).start())
+    for d in (3, 5):
+        pass_on(d)
     to_tiles(lambda t: link(block_of(vs, t), head_rows(vt), V, img, t).start())
-
-    own = wall.at[c, sigma]
-    lower, upper = wall.at[c, sigma, 0:4], wall.at[c, sigma, 4:8]
-    other = tile + 1 - 2 * c
-    arrived(wall.at[0, 0, 0:7], W1)
-    link(own, own, W2, along(1), tile).start()
-    link(own, own, W2, along(7), tile).start()
-    link(lower, lower, W2, along(2), tile).start()
-    link(upper, upper, W2, along(6), tile).start()
-    link(own, own, W3, img, other).start()
-    arrived(wall.at[0, 0:3], W2)
-    for i in range(1, 4):
-        more = wall.at[c, (sigma + i) % 4]
-        link(more, more, W3, img, other).start()
-
+    pass_on(4)
+
+    loads[5].wait()
     hidden = h_ref[...].astype(F32)
     inverse = lax.rsqrt(jnp.mean(hidden * hidden, axis=1, keepdims=True) + NORM_EPS)
     normed = hidden * inverse
@@ -200,7 +236,7 @@
     upstream = jnp.concatenate(halves, axis=1)
     both = upstream * normed
     part_sum = jnp.sum(both, axis=0, keepdims=True)
-    gain = gain_ref[...]
+    gain = gain_ref[...].reshape(1, D)
     mean = jnp.mean(gain * both, axis=1, keepdims=True)
     attn = (inverse * (gain * upstream - normed * mean)).astype(BF16)
     g1s[...] = part_sum
@@ -212,18 +248,30 @@
             acc = jnp.zeros((384, ROWS), F32)
             for dh in range(2):
                 acc = acc + dot(
-                    wall[c2, ch * 2 + dh].reshape(384, HALF), attn[:, dh * HALF : (dh + 1) * HALF], 1, 1
+                    wall[c2, 2 * (ch * 2 + dh) : 2 * (ch * 2 + dh) + 2].reshape(384, HALF), attn[:, dh * HALF : (dh + 1) * HALF], 1, 1
                 )
             acc = acc.astype(BF16)
             for y2 in range(8):
-                base = (2 * y2 + c2) * HEAD
+                base = (2 * (2 * (y2 % 4) + y2 // 4) + c2) * HEAD
                 if ch == 0:
                     gs[base : base + 48, :] = acc[48 * y2 : 48 * y2 + 48]
                 else:
                     gs[base + 48 : base + 80, :] = acc[48 * y2 + 16 : 48 * y2 + 48]
     gt[0:HEAD, pl.ds(me128, ROWS)] = gs[pl.ds(me80, HEAD), :]
     to_tiles(lambda t: link(g1s, g1.at[tile], GA, img, t).start())
-    to_tiles(lambda t: link(block_of(gs, t), head_rows(gt), G, img, t).start())
+
+    def turn(i):
+        return (8 + ((i + 1) // 2) * (2 * (i % 2) - 1)) % 8
+
+    def send_g(i, carry):
+        o = turn(i)
+        for core in range(2):
+            t = 2 * ((y + o) % 8) + core
+            link(block_of(gs, t), head_rows(gt), G + (8 - o) % 8, img, t).start()
+        return carry
+
+    link(block_of(gs, other), head_rows(gt), G, img, other).start()
+    lax.fori_loop(1, 8, send_g, 0)
 
     arrived(qt.at[0:HEAD, 0 : PATCHES - ROWS], Q)
     arrived(kt.at[0:HEAD, 0 : PATCHES - ROWS], K)
@@ -253,37 +301,60 @@
         return carry
 
     lax.fori_loop(1, 8, send_g2, 0)
-    arrived(gt.at[0:HEAD, 0 : PATCHES - ROWS], G)
-
-    def backward(j, carry):
+
+    def columns(ref, t):
+        return ref.at[:, pl.ds(pl.multiple_of(t * ROWS, ROWS), ROWS)]
+
+    def back(src, dst, kind, t):
+        link(columns(src, t), block_of(dst, tile), kind, img, t).start()
+
+    def hand_back(src, dst, kind, i, j):
+        @pl.when(i > 0)
+        def _():
+            back(src, dst, kind, 2 * j)
+            back(src, dst, kind, 2 * j + 1)
+
+        @pl.when(i == 0)
+        def _():
+            back(src, dst, kind, other)
+            dst[pl.ds(me80, HEAD), :] = src[:, pl.ds(me128, ROWS)]
+
+    def backward(i, carry):
+        j = (y + turn(i)) % 8
+
+        @pl.when(i == 0)
+        def _():
+            arrived(gt.at[0:HEAD, 0:ROWS], G)
+
+        @pl.when(i > 0)
+        def _():
+            arrived(gt.at[0:HEAD, 0:QB], G + turn(i))
+
         at = pl.ds(pl.multiple_of(j * QB, QB), QB)
-        grads = gt[:, at]
-        dprobs = dot(grads.T, vt[...], 1, 0)
-        low = probs[at, :]
-        weight = low.astype(F32)
+        dprobs = dot(gt[:, at].T, vt[...], 1, 0)
+        weight = probs[at, :].astype(F32)
         prod = weight * dprobs
         spread = jnp.sum(prod, axis=1, keepdims=True)
         dscores = (prod - weight * spread).astype(BF16)
-        dv[...] += dot(grads[0:HEAD], low, 1, 0)
         dk[...] += dot(qt[0:HEAD, at], dscores, 1, 0)
         dq = dot(kt[0:HEAD, :], dscores, 1, 1)
         dqb[:, at] = (dq * FACTOR).astype(BF16)
-        return carry
-
-    lax.fori_loop(0, PATCHES // QB, backward, 0)
-
-    def columns(ref, t):
-        return ref.at[:, pl.ds(pl.multiple_of(t * ROWS, ROWS), ROWS)]
-
-    def back(src, dst, kind):
-        dst[pl.ds(me80, HEAD), :] = src[:, pl.ds(me128, ROWS)]
-        to_tiles(lambda t: link(columns(src, t), block_of(dst, tile), kind, img, t).start())
-
-    dvb[...] = dv[...].astype(BF16)
+        hand_back(dqb, bq, DQ, i, j)
+        return carry
+
+    lax.fori_loop(0, 8, backward, 0)
     dkb[...] = (dk[...] * FACTOR).astype(BF16)
-    back(dqb, bq, DQ)
-    back(dvb, bv, DV)
-    back(dkb, bk, DK)
+    bk[pl.ds(me80, HEAD), :] = dkb[:, pl.ds(me128, ROWS)]
+    to_tiles(lambda t: back(dkb, bk, DK, t))
+
+    def value_grads(i, carry):
+        j = (y + turn(i)) % 8
+        at = pl.ds(pl.multiple_of(j * QB, QB), QB)
+        dvb[:, at] = dot(gt[0:HEAD, :], probs[:, at], 1, 0).astype(BF16)
+        hand_back(dvb, bv, DV, i, j)
+        return carry
+
+    lax.fori_loop(0, 8, value_grads, 0)
 
     arrived(g2.at[0:7], GB)
     total = g2[0]
@@ -303,45 +374,77 @@
         total = total + g3[i]
     og_ref[...] = total
 
-    for src, dst, kind in ((bq, oq_ref, DQ), (bv, ov_ref, DV), (bk, ok_ref, DK)):
+    stores = []
+    for i, (src, kind) in enumerate(((bq, DQ), (bk, DK), (bv, DV))):
         arrived(src.at[0 : D - HEAD], kind)
-        for b in range(10):
-            dst[:, b * 128 : (b + 1) * 128] = src[b * 128 : (b + 1) * 128, :].T
+        stores.append(pltpu.make_async_copy(src, out_hbm.at[i], lsem.at[i]))
+        stores[-1].start()
+    for store in stores:
+        store.wait()
 
     sent(reqr.at[0 : T - 1], REQ)
-    sent(wall.at[0, 0, 0:7], W1)
-    sent(wall.at[0, 0:3], W2)
+
+    @pl.when(mine_too)
+    def _():
+        sent(wall.at[0, 0:7, 0], W1)
+
+    for d in range(1, 8):
+        sent(wall.at[0, 0], W2 + d)
     sent(wall.at[0], W3)
     sent(rsend.at[0 : T - 1], ROW)
-    for kind in (Q, K, V, G, DQ, DK, DV):
+    for kind in (Q, K, V, DQ, DK, DV):
         sent(qs.at[0 : D - HEAD], kind)
+    sent(qs.at[0:HEAD], G)
+    for o in range(1, 8):
+        sent(qs.at[0 : 2 * HEAD], G + o)
     sent(g1.at[0 : T - 1], GA)
     sent(g2.at[0:7], GB)
     sent(g3.at[0:7], GC)
 
 
+def finish(in_hbm, g_ref, oq_hbm, ok_hbm, ov_hbm, og_ref, taken, turned, isem, osem):
+    loads = [pltpu.make_async_copy(in_hbm.at[i], taken.at[i], isem.at[i]) for i in range(3)]
+    for load in loads:
+        load.start()
+    og_ref[...] = g_ref[...].reshape(D)
+    stores = []
+    for i, out in enumerate((oq_hbm, ok_hbm, ov_hbm)):
+        loads[i].wait()
+        for b in range(10):
+            turned[i, :, b * 128 : (b + 1) * 128] = taken[i, b * 128 : (b + 1) * 128, :].T
+        stores.append(pltpu.make_async_copy(turned.at[i], out, osem.at[i]))
+        stores[-1].start()
+    for store in stores:
+        store.wait()
+
+
 def body(query, keys, values, out_weight, hidden, gain, seq_grad, splice_at, merged_count):
     smem = pl.BlockSpec(memory_space=pltpu.SMEM)
     vmem = pl.BlockSpec(memory_space=pltpu.VMEM)
+    hbm = pl.BlockSpec(memory_space=pl.ANY)
     block = jax.ShapeDtypeStruct((ROWS, D), BF16)
     head = pltpu.VMEM((128, PATCHES), BF16)
+    flat = pltpu.VMEM((ROWS, D), BF16)
     blocks = pltpu.VMEM((D, ROWS), BF16)
-    grads = pl.pallas_call(
+    grads, gain_grad = pl.pallas_call(
         kernel,
-        out_shape=(block, block, block, jax.ShapeDtypeStruct((1, D), F32)),
-        in_specs=[smem, smem] + [vmem] * 7,
-        out_specs=(vmem,) * 4,
+        out_shape=(jax.ShapeDtypeStruct((3, D, ROWS), BF16), jax.ShapeDtypeStruct((1, D), F32)),
+        in_specs=[smem, vmem, vmem] + [hbm] * 6,
+        out_specs=(hbm, vmem),
         scratch_shapes=[
+            *[flat] * 3,
+            pltpu.VMEM((HEAD, D), BF16),
+            flat,
+            pltpu.VMEM((ROWS, 4 * D), BF16),
             *[blocks] * 4,
             *[head] * 4,
-            pltpu.VMEM((2, 4, 8, 48, HALF), BF16),
+            pltpu.VMEM((2, 8, 4, 48, HALF), BF16),
             pltpu.VMEM((4, 1, 128), jnp.int32),
             pltpu.VMEM((T, 1, 128), jnp.int32),
             pltpu.VMEM((128, 128), F32),
             pltpu.VMEM((T, 32, HALF), BF16),
             pltpu.VMEM((T, 32, HALF), BF16),
             pltpu.VMEM((PATCHES, PATCHES), BF16),
-            pltpu.VMEM((HEAD, PATCHES), F32),
             pltpu.VMEM((HEAD, PATCHES), F32),
             *[pltpu.VMEM((HEAD, PATCHES), BF16)] * 3,
             *[blocks] * 3,
@@ -351,8 +454,9 @@
             pltpu.VMEM((8, 1, D), F32),
             pltpu.VMEM((1, D), F32),
             pltpu.VMEM((8, 1, D), F32),
-            pltpu.SemaphoreType.DMA((15,)),
-            pltpu.SemaphoreType.DMA((15,)),
+            pltpu.SemaphoreType.DMA((29,)),
+            pltpu.SemaphoreType.DMA((29,)),
+            pltpu.SemaphoreType.DMA((6,)),
         ],
         compiler_params=pltpu.CompilerParams(
             collective_id=0, has_side_effects=True, vmem_limit_bytes=60 * 1024 * 1024
@@ -360,15 +464,27 @@
     )(
         splice_at,
         merged_count,
+        gain,
         query[0],
         keys[0],
         values[0],
         out_weight,
         hidden[0],
-        gain[None, :],
         seq_grad[0],
     )
-    return grads[0][None], grads[1][None], grads[2][None], grads[3][0]
+    oq, ok, ov, og = pl.pallas_call(
+        finish,
+        out_shape=(block, block, block, jax.ShapeDtypeStruct((D,), F32)),
+        in_specs=[hbm, vmem],
+        out_specs=(hbm, hbm, hbm, vmem),
+        scratch_shapes=[
+            pltpu.VMEM((3, D, ROWS), BF16),
+            pltpu.VMEM((3, ROWS, D), BF16),
+            pltpu.SemaphoreType.DMA((3,)),
+            pltpu.SemaphoreType.DMA((3,)),
+        ],
+    )(grads, gain_grad)
+    return oq[None], ok[None], ov[None], og
 
 
 def solution(mesh):

time: 126 us -> 110 us (0.87); the launches traced: 126 us -> 108 us
  Pallas kernels: 118 us -> 107 us
  local copies, waits for them, and re-layouts: 5.46 us -> 0 us
  other arithmetic: 1.35 us -> 0 us
    pallas_call x1 -> x2, Pallas kernels: 118 us -> 107 us  [the longest x1 103 us: body(): pl.pallas_call(kernel, out_shape=(jax.ShapeDtypeStruct((3, D, ROWS), BF16...]
    unnamed x5 -> x0, local copies, waits for them, and re-layouts: 4.16 us -> none
    pallas_call x1 -> x0, other arithmetic: 1.35 us -> none  [body(): pl.pallas_call(kernel, out_shape=(block, block, block, jax.ShapeDtypeStru...]
    broadcast_in_dim x1 -> x0, local copies, waits for them, and re-layouts: 1.29 us -> none  [body(): gain[None, :]]
where the time goes in v2:
time: 110 us; the launch traced here: 108 us
  Pallas kernels  107 us (97%)
  between operations  1.29 us (1%)
    pallas_call x1, Pallas kernels, body(): pl.pallas_call(kernel, out_shape=(jax.ShapeDtypeStruct((3, D, ROWS), BF16...  103 us
    pallas_call x1, Pallas kernels, body(): pl.pallas_call(finish, out_shape=(block, block, block, jax.ShapeDtypeStru...  3.45 us

profile of v2, /device:TPU:1, one launch (start us, length us, event | category | flops | bytes accessed | tf_op | source)
XLA Modules:
  0.0 108.1 jit_solution(8703551183955544169)
XLA Ops:
  1.3 103.4 %shard_map.120 = (bf16[3,1280,128]{2,1,0:T(8,128)(2,1)}, f32[1,1280]{1,0:T(1,128)}) custom-call(s32[1,32]{1,0:T(1,128)} %pos_ref.1, s32[1]{0:T(128)S(6)} %copy.13.count_ref, f32[1280]{0:T(1024)} %gain_ref.1, bf16[128,1280]{1,0:T(8,128)(2,1)} %bitcast.9, bf16[128,1280]{1,0:T(8,128)(2,1)} %bitcast.10, bf16[128,1280]{1,0:T(8,128)(2,1)} %bitcast.11, ...), custom_call_target="tpu_custom_call" | custom-call | tf_op jit(solution)/shard_map/pallas_call | solution.py:429
  104.7 3.5 %shard_map.121 = (bf16[128,1280]{1,0:T(8,128)(2,1)}, bf16[128,1280]{1,0:T(8,128)(2,1)}, bf16[128,1280]{1,0:T(8,128)(2,1)}, f32[1280]{0:T(1024)}) custom-call(bf16[3,1280,128]{2,1,0:T(8,128)(2,1)} %get-tuple-element.10.in_hbm, f32[1,1280]{1,0:T(1,128)} %get-tuple-element.11.g_ref), custom_call_target="tpu_custom_call" | custom-call | tf_op jit(solution)/shard_map/pallas_call | solution.py:475
